TPU v7x, 32 devices: a whole 2x2x4 slice. The times are simulated.
32 devices in a mesh: pb: 4 (over z), ka: 8 (over y, x, core).
Axes of the slice: x: 2, y: 2, z: 4, core: 2. Of those that a mesh axis runs over, the one named last changes fastest.
Arguments:
- queries: float32 [1, 4096, 128], P(None, ('pb', 'ka')), may hold values from -6 to 6
- keys: float32 [1, 4096, 128], P(None, ('ka', 'pb')), may hold values from -6 to 6
- values: float32 [1, 4096, 128], P(None, ('ka', 'pb')), may hold values from -6 to 6
- tangent_q: float32 [1, 4096, 128], P(None, ('pb', 'ka')), may hold values from -6 to 6
- tangent_k: float32 [1, 4096, 128], P(None, ('ka', 'pb')), may hold values from -6 to 6
- tangent_v: float32 [1, 4096, 128], P(None, ('ka', 'pb')), may hold values from -6 to 6
Outputs:
- attended: float32 [1, 4096, 128], P(None, ('pb', 'ka'))
- attended_tangent: float32 [1, 4096, 128], P(None, ('pb', 'ka'))
All inputs are finite; a program needn't handle non-finite values.
Results may differ from a plain program's by a relative error of at most 0.0003.
Values sent between devices are 32-bit elements; how exact they have to be, the bound alone decides.
No kernel may reach another device: no remote copies, remote signals or barrier semaphores. Data moves between devices by JAX's collectives and lax.ppermute only.
A program may use at most 128 MiB of HBM per device.

v0:
```python
import jax
import jax.numpy as jnp
from jax import lax
from jax.sharding import PartitionSpec as P


def combined_all(value, axis, join):
    pieces = jax.tree.map(lambda part: lax.all_gather(part, axis), value)
    head = jax.tree.map(lambda part: part[0], pieces)
    tail = jax.tree.map(lambda part: part[1:], pieces)
    so_far, _ = lax.scan(lambda so_far, share: (join(so_far, share), None), head, tail)
    return so_far


def join_partials(first, second):
    peak = jnp.maximum(first[0], second[0])
    left = jnp.exp(first[0] - peak)
    right = jnp.exp(second[0] - peak)
    total = first[1] * left + second[1] * right
    numer = first[2] * left[..., None] + second[2] * right[..., None]
    tnumer = first[3] * left[..., None] + second[3] * right[..., None]
    drift = first[4] * left + second[4] * right
    return (peak, total, numer, tnumer, drift)


def body(queries, keys, values, tangent_q, tangent_k, tangent_v):
    highest = lax.Precision.HIGHEST
    head_count, _, width = queries.shape
    factor = width ** (-0.5)
    all_q, all_dq = (
        lax.all_gather(queries, "ka", axis=1, tiled=True),
        lax.all_gather(tangent_q, "ka", axis=1, tiled=True),
    )
    span = all_q.shape[1]
    block = min(512, span)
    blocks = span // block
    split_q = all_q.reshape(head_count, blocks, block, width)
    split_dq = all_dq.reshape(head_count, blocks, block, width)
    start_state = (
        jnp.full((head_count, span), -1e30, jnp.float32),
        jnp.zeros((head_count, span), jnp.float32),
        jnp.zeros((head_count, span, width), jnp.float32),
        jnp.zeros((head_count, span, width), jnp.float32),
        jnp.zeros((head_count, span), jnp.float32),
    )
    piece_k = lax.all_gather(keys, "pb", axis=1, tiled=True)
    piece_dk = lax.all_gather(tangent_k, "pb", axis=1, tiled=True)
    piece_v = lax.all_gather(values, "pb", axis=1, tiled=True)
    piece_dv = lax.all_gather(tangent_v, "pb", axis=1, tiled=True)
    shaped = (
        start_state[0].reshape(head_count, blocks, block),
        start_state[1].reshape(head_count, blocks, block),
        start_state[2].reshape(head_count, blocks, block, width),
        start_state[3].reshape(head_count, blocks, block, width),
        start_state[4].reshape(head_count, blocks, block),
    )

    def one_head(items):
        (
            head_q,
            head_dq,
            head_k,
            head_dk,
            head_v,
            head_dv,
            peak_h,
            total_h,
            numer_h,
            tnumer_h,
            drift_h,
        ) = items

        def one_block(parts):
            query_blk, dquery_blk, old_peak, old_total, old_numer, old_tnumer, old_drift = parts
            scores = jnp.dot(query_blk, head_k.T, precision=highest) * factor
            tangent = (
                jnp.dot(dquery_blk, head_k.T, precision=highest)
                + jnp.dot(query_blk, head_dk.T, precision=highest)
            ) * factor
            new_peak = jnp.maximum(old_peak, jnp.max(scores, axis=1))
            rescale = jnp.exp(old_peak - new_peak)
            weights = jnp.exp(scores - new_peak[:, None])
            product = weights * tangent
            new_total = old_total * rescale + jnp.sum(weights, axis=1)
            new_numer = old_numer * rescale[:, None] + jnp.dot(weights, head_v, precision=highest)
            new_tnumer = (
                old_tnumer * rescale[:, None]
                + jnp.dot(weights, head_dv, precision=highest)
                + jnp.dot(product, head_v, precision=highest)
            )
            new_drift = old_drift * rescale + jnp.sum(product, axis=1)
            return (new_peak, new_total, new_numer, new_tnumer, new_drift)

        return lax.map(one_block, (head_q, head_dq, peak_h, total_h, numer_h, tnumer_h, drift_h))

    result = lax.map(one_head, (split_q, split_dq, piece_k, piece_dk, piece_v, piece_dv) + shaped)
    peak = result[0].reshape(head_count, span)
    total = result[1].reshape(head_count, span)
    numer = result[2].reshape(head_count, span, width)
    tnumer = result[3].reshape(head_count, span, width)
    drift = result[4].reshape(head_count, span)
    merged = combined_all((peak, total, numer, tnumer, drift), "ka", join_partials)
    owned = span // lax.axis_size("ka")
    offset = lax.axis_index("ka") * owned
    total = lax.dynamic_slice_in_dim(merged[1], offset, owned, 1)
    numer = lax.dynamic_slice_in_dim(merged[2], offset, owned, 1)
    tnumer = lax.dynamic_slice_in_dim(merged[3], offset, owned, 1)
    drift = lax.dynamic_slice_in_dim(merged[4], offset, owned, 1)
    attended = numer / total[..., None]
    attended_tangent = tnumer / total[..., None] - attended * (drift / total)[..., None]
    return (attended, attended_tangent)


def solution(mesh):
    return jax.shard_map(
        body,
        mesh=mesh,
        in_specs=(
            P(None, ("pb", "ka"), None),
            P(None, ("ka", "pb"), None),
            P(None, ("ka", "pb"), None),
            P(None, ("pb", "ka"), None),
            P(None, ("ka", "pb"), None),
            P(None, ("ka", "pb"), None),
        ),
        out_specs=(P(None, ("pb", "ka"), None), P(None, ("pb", "ka"), None)),
        check_vma=False,
    )
```

profile of v0, /device:TPU:0, one launch (start us, length us, event | category | flops | bytes accessed | tf_op | source)
XLA Modules:
  0.0 214.0 jit_solution(3527905628978141757)
XLA Ops:
  7.3 15.9 %all_gather.34 = f32[1,512,128]{2,1,0:T(8,128)S(1)} all-gather(f32[1,128,128]{2,1,0:T(8,128)} %param.11), channel_id=1, replica_groups=mesh['pb'=4,'ka'=8] {'pb'}, dimensions={1}, use_global_device_ids=true | all-gather | bytes 327680 | tf_op jit(solution)/shard_map/all_gather | solution.py:46
  23.1 14.9 %all_gather.35 = f32[1,512,128]{2,1,0:T(8,128)S(1)} all-gather(f32[1,128,128]{2,1,0:T(8,128)} %param.12), channel_id=1, replica_groups=mesh['pb'=4,'ka'=8] {'pb'}, dimensions={1}, use_global_device_ids=true | all-gather | bytes 327680 | tf_op jit(solution)/shard_map/all_gather | solution.py:48
  38.0 14.0 %all_gather.38 = f32[1,512,128]{2,1,0:T(8,128)S(1)} all-gather(f32[1,128,128]{2,1,0:T(8,128)} %param.14), channel_id=1, replica_groups=mesh['pb'=4,'ka'=8] {'pb'}, dimensions={1}, use_global_device_ids=true | all-gather | bytes 327680 | tf_op jit(solution)/shard_map/all_gather | solution.py:47
  52.1 16.6 %all_gather.36 = f32[1,512,128]{2,1,0:T(8,128)} all-gather(f32[1,128,128]{2,1,0:T(8,128)} %param.15), channel_id=1, replica_groups=mesh['pb'=4,'ka'=8] {'pb'}, dimensions={1}, use_global_device_ids=true | all-gather | bytes 327680 | tf_op jit(solution)/shard_map/all_gather | solution.py:49
  68.6 10.1 %all_gather.33 = f32[1,1024,128]{2,1,0:T(8,128)S(1)} all-gather(f32[1,128,128]{2,1,0:T(8,128)} %param.10), channel_id=1, replica_groups=mesh['pb'=4,'ka'=8] {'ka'}, dimensions={1}, use_global_device_ids=true | all-gather | bytes 589824 | tf_op jit(solution)/shard_map/all_gather | solution.py:31
  78.8 10.8 %all_gather.37 = f32[1,1024,128]{2,1,0:T(8,128)} all-gather(f32[1,128,128]{2,1,0:T(8,128)} %param.13), channel_id=1, replica_groups=mesh['pb'=4,'ka'=8] {'ka'}, dimensions={1}, use_global_device_ids=true | all-gather | bytes 589824 | tf_op jit(solution)/shard_map/all_gather | solution.py:32
  89.5 24.6 %while.53 = (s32[]{:T(128)}, f32[2,512]{1,0:T(2,128)S(1)}, f32[2,512]{1,0:T(2,128)S(1)}, f32[2,512,128]{2,1,0:T(8,128)}, f32[2,512,128]{2,1,0:T(8,128)}, /*index...) while((s32[]{:T(128)}, f32[2,512]{1,0:T(2,128)S(1)}, ...), condition=%wide.region_4.5_spmd, body=%wide.region_0.4_spmd.sunk | while | flops 2419001344 | bytes 12892333 | solution.py:94
  89.5 1.9 fusion.66
  92.7 1.2 fusion.67
  94.0 2.8 %convolution_add_fusion.5 = f32[512,128]{1,0:T(8,128)S(1)} fusion(f32[512,128]{1,0:T(8,128)} %get-tuple-element.549, f32[512,512]{0,1:T(8,128)S(1)} %get-tuple-element.489, f32[512]{0:T(512)S(1)} %get-tuple-element.488, f32[512]{0:T(512)S(1)} %get-tuple-element.492), kind=kOutput, calls=%fused_computation.7.clone.1 | convolution fusion | flops 402980864 | bytes 1576960 | tf_op jit(solution)/shard_map/while/body/eval_jaxpr/while/body/eval_jaxpr/dot_general | solution.py:88
  96.8 2.5 %fusion.71 = f32[2,512,128]{2,1,0:T(8,128)} fusion(f32[2,512,128]{2,1,0:T(8,128)} %get-tuple-element.530, s32[]{:T(128)S(6)} %copy.19, f32[512,128]{1,0:T(8,128)S(1)} %convolution_add_fusion.5, f32[512,512]{0,1:T(8,128)S(1)} %get-tuple-element.493, f32[512,128]{1,0:T(8,128)S(1)} %get-tuple-element.548), kind=kOutput, calls=%fused_computation.6.clone.1 | convolution fusion | flops 402718720 | bytes 1835012 | tf_op jit(solution)/shard_map/while/body/eval_jaxpr/while/body/eval_jaxpr/dot_general | solution.py:89
  99.3 2.5 %fusion.70 = f32[2,512,128]{2,1,0:T(8,128)} fusion(f32[2,512,128]{2,1,0:T(8,128)} %get-tuple-element.529, s32[]{:T(128)S(6)} %copy.19, f32[512,128]{1,0:T(8,128)S(1)} %get-tuple-element.548, f32[512,512]{0,1:T(8,128)S(1)} %get-tuple-element.489, f32[512]{0:T(512)S(1)} %get-tuple-element.488, f32[512]{0:T(512)S(1)} %get-tuple-element.492), kind=kOutput, calls=%fused_computation.10.clone.1 | convolution fusion | flops 402980864 | bytes 1576964 | tf_op jit(solution)/shard_map/while/body/eval_jaxpr/while/body/eval_jaxpr/dot_general | solution.py:85
  101.9 1.9 fusion.66
  105.1 1.2 fusion.67
  106.4 2.8 %convolution_add_fusion.5 = f32[512,128]{1,0:T(8,128)S(1)} fusion(f32[512,128]{1,0:T(8,128)} %get-tuple-element.549, f32[512,512]{0,1:T(8,128)S(1)} %get-tuple-element.489, f32[512]{0:T(512)S(1)} %get-tuple-element.488, f32[512]{0:T(512)S(1)} %get-tuple-element.492), kind=kOutput, calls=%fused_computation.7.clone.1 | convolution fusion | flops 402980864 | bytes 1576960 | tf_op jit(solution)/shard_map/while/body/eval_jaxpr/while/body/eval_jaxpr/dot_general | solution.py:88
  109.1 2.5 %fusion.71 = f32[2,512,128]{2,1,0:T(8,128)} fusion(f32[2,512,128]{2,1,0:T(8,128)} %get-tuple-element.530, s32[]{:T(128)S(6)} %copy.19, f32[512,128]{1,0:T(8,128)S(1)} %convolution_add_fusion.5, f32[512,512]{0,1:T(8,128)S(1)} %get-tuple-element.493, f32[512,128]{1,0:T(8,128)S(1)} %get-tuple-element.548), kind=kOutput, calls=%fused_computation.6.clone.1 | convolution fusion | flops 402718720 | bytes 1835012 | tf_op jit(solution)/shard_map/while/body/eval_jaxpr/while/body/eval_jaxpr/dot_general | solution.py:89
  111.7 2.5 %fusion.70 = f32[2,512,128]{2,1,0:T(8,128)} fusion(f32[2,512,128]{2,1,0:T(8,128)} %get-tuple-element.529, s32[]{:T(128)S(6)} %copy.19, f32[512,128]{1,0:T(8,128)S(1)} %get-tuple-element.548, f32[512,512]{0,1:T(8,128)S(1)} %get-tuple-element.489, f32[512]{0:T(512)S(1)} %get-tuple-element.488, f32[512]{0:T(512)S(1)} %get-tuple-element.492), kind=kOutput, calls=%fused_computation.10.clone.1 | convolution fusion | flops 402980864 | bytes 1576964 | tf_op jit(solution)/shard_map/while/body/eval_jaxpr/while/body/eval_jaxpr/dot_general | solution.py:85
  115.0 8.8 %all_gather.40 = f32[8,1,1024]{2,1,0:T(1,128)S(1)} all-gather(f32[1,1,1024]{2,1,0:T(1,128)S(1)} %all_gather_reshape.16), channel_id=1, replica_groups=mesh['pb'=4,'ka'=8] {'ka'}, dimensions={0}, use_global_device_ids=true | all-gather | bytes 36864 | tf_op jit(solution)/shard_map/all_gather | solution.py:8
  123.8 8.6 %all_gather.39 = f32[8,1,1024]{2,1,0:T(1,128)S(1)} all-gather(f32[1,1,1024]{2,1,0:T(1,128)S(1)} %all_gather_reshape.15), channel_id=1, replica_groups=mesh['pb'=4,'ka'=8] {'ka'}, dimensions={0}, use_global_device_ids=true | all-gather | bytes 36864 | tf_op jit(solution)/shard_map/all_gather | solution.py:8
  132.4 9.0 %all_gather.43 = f32[8,1,1024]{2,1,0:T(1,128)S(1)} all-gather(f32[1,1,1024]{2,1,0:T(1,128)S(1)} %all_gather_reshape.19), channel_id=1, replica_groups=mesh['pb'=4,'ka'=8] {'ka'}, dimensions={0}, use_global_device_ids=true | all-gather | bytes 36864 | tf_op jit(solution)/shard_map/all_gather | solution.py:8
  141.4 8.8 %all-gather.5.cloned.1.call-done = f32[8,1,1024,128]{3,2,1,0:T(8,128)} async-done(((f32[1,1,1024,128]{3,2,1,0:T(8,128)}), f32[8,1,1024,128]{3,2,1,0:T(8,128)}) %all-gather.5.cloned.1.call-update) | async-done | bytes 4194320 | tf_op jit(solution)/shard_map/all_gather | solution.py:8
  150.2 4.1 %slice.48 = f32[7,1,1024,128]{3,2,1,0:T(8,128)} slice(f32[8,1,1024,128]{3,2,1,0:T(8,128)} %all-gather.5.cloned.1.call-done), slice={[1:8], [0:1], [0:1024], [0:128]} | slice | bytes 7340032 | tf_op jit(solution)/shard_map/slice | solution.py:10
  155.4 33.3 %all-gather.3.cloned.1.call-done = f32[8,1,1024,128]{3,2,1,0:T(8,128)} async-done(((f32[1,1,1024,128]{3,2,1,0:T(8,128)}), f32[8,1,1024,128]{3,2,1,0:T(8,128)}) %all-gather.3.cloned.1.call-update) | async-done | bytes 4194320 | tf_op jit(solution)/shard_map/all_gather | solution.py:8
  189.8 4.1 %slice.47 = f32[7,1,1024,128]{3,2,1,0:T(8,128)} slice(f32[8,1,1024,128]{3,2,1,0:T(8,128)} %all-gather.3.cloned.1.call-done), slice={[1:8], [0:1], [0:1024], [0:128]} | slice | bytes 7340032 | tf_op jit(solution)/shard_map/slice | solution.py:10
  193.8 12.5 %while.54 = (s32[]{:T(128)}, f32[1,1024]{1,0:T(1,128)S(1)}, f32[1,1024]{1,0:T(1,128)S(1)}, f32[1,1024,128]{2,1,0:T(8,128)S(1)}, f32[1,1024,128]{2,1,0:T(8,128)S(...) while((s32[]{:T(128)}, f32[1,1024]{1,0:T(1,128)S(1)}, ...), condition=%wide.region_6.7_spmd, body=%wide.region_5.6_spmd.sunk | while | flops 795650 | bytes 3207305 | solution.py:11
  193.9 1.7 fusion.74
  195.7 1.7 fusion.74
  197.5 1.7 fusion.74
  199.3 1.7 fusion.74
  201.1 1.7 fusion.74
  202.9 1.7 fusion.74
  204.7 1.7 fusion.74
  (59 shorter events, 7.0 us)
Async XLA Ops:
  7.2 143.0 %all-gather.5.cloned.1.call-start = ((), (), s32[]{:S(2)}) async-start(), calls=%async_computation.1 | async-start | bytes 4718592 | tf_op jit(solution)/shard_map/all_gather | solution.py:8
  114.2 74.5 %all-gather.3.cloned.1.call-start = ((), (), s32[]{:S(2)}) async-start(), calls=%async_computation | async-start | bytes 4718592 | tf_op jit(solution)/shard_map/all_gather | solution.py:8
  123.8 31.5 %copy-start = (f32[8,1,1024]{2,1,0:T(1,128)}, f32[8,1,1024]{2,1,0:T(1,128)S(1)}, u32[]{:S(2)}) copy-start(f32[8,1,1024]{2,1,0:T(1,128)S(1)} %all_gather.40) | copy-start | bytes 98308
  132.4 22.9 %copy-start.1 = (f32[8,1,1024]{2,1,0:T(1,128)}, f32[8,1,1024]{2,1,0:T(1,128)S(1)}, u32[]{:S(2)}) copy-start(f32[8,1,1024]{2,1,0:T(1,128)S(1)} %all_gather.39) | copy-start | bytes 98308
  141.4 13.9 %copy-start.2 = (f32[8,1,1024]{2,1,0:T(1,128)}, f32[8,1,1024]{2,1,0:T(1,128)S(1)}, u32[]{:S(2)}) copy-start(f32[8,1,1024]{2,1,0:T(1,128)S(1)} %all_gather.43) | copy-start | bytes 98308
  188.7 5.2 %slice-start = ((f32[8,1,1024]{2,1,0:T(1,128)}), f32[7,1,1024]{2,1,0:T(1,128)S(1)}, s32[]{:S(2)}) async-start(f32[8,1,1024]{2,1,0:T(1,128)} %copy-done), calls=%async_computation.2 | async-start | bytes 57344 | tf_op jit(solution)/shard_map/slice | solution.py:10
  188.7 5.2 %slice-start.1 = ((f32[8,1,1024]{2,1,0:T(1,128)}), f32[7,1,1024]{2,1,0:T(1,128)S(1)}, s32[]{:S(2)}) async-start(f32[8,1,1024]{2,1,0:T(1,128)} %copy-done.1), calls=%async_computation.3 | async-start | bytes 57344 | tf_op jit(solution)/shard_map/slice | solution.py:10
  188.7 5.2 %slice-start.2 = ((f32[8,1,1024]{2,1,0:T(1,128)}), f32[7,1,1024]{2,1,0:T(1,128)S(1)}, s32[]{:S(2)}) async-start(f32[8,1,1024]{2,1,0:T(1,128)} %copy-done.2), calls=%async_computation.4 | async-start | bytes 57344 | tf_op jit(solution)/shard_map/slice | solution.py:10
Sparse Core Ops, SparseCore 0:
  114.3 35.8 all-gather.4
  152.1 36.5 all-gather.2
where the time goes:
time: 215 us; the launch traced here: 214 us
  blocking collectives  109 us (51%)
  waiting for transfers between devices  42.8 us (20%)
  matrix products  23.9 us (11%)
  between operations  14.1 us (7%)
  other arithmetic  13.6 us (6%)
  local copies, waits for them, and re-layouts  10.6 us (5%)
    all_gather x2, waiting for transfers between devices, combined_all(): pieces = jax.tree.map(lambda part: lax.all_gather(part, axis), value)  42.1 us
    all_gather x3, blocking collectives, combined_all(): pieces = jax.tree.map(lambda part: lax.all_gather(part, axis), value)  26.4 us
    all_gather x1, blocking collectives, body(): piece_dv = lax.all_gather(tangent_v, 'pb', axis=1, tiled=True)  16.6 us
    all_gather x1, blocking collectives, body(): piece_k = lax.all_gather(keys, 'pb', axis=1, tiled=True)  15.9 us
    all_gather x1, blocking collectives, body(): piece_v = lax.all_gather(values, 'pb', axis=1, tiled=True)  14.9 us
    all_gather x1, blocking collectives, body(): piece_dk = lax.all_gather(tangent_k, 'pb', axis=1, tiled=True)  14 us
    add x7, other arithmetic, join_partials(): tnumer = first[3] * left[..., None] + second[3] * right[..., None]  11.9 us
    all_gather x1, blocking collectives, body(): lax.all_gather(tangent_q, 'ka', axis=1, tiled=True)  10.8 us
  transfers between devices with their start and end apart: 2, of which 2 were waited for; matrix products, arithmetic and copies ran while one was open for 2% of the time, Pallas kernels for 0%

commit v1 on v0

--- a/solution.py
+++ b/solution.py
@@ -43,8 +43,11 @@
         jnp.zeros((head_count, span, width), jnp.float32),
         jnp.zeros((head_count, span), jnp.float32),
     )
-    piece_k = lax.all_gather(keys, "pb", axis=1, tiled=True)
-    piece_dk = lax.all_gather(tangent_k, "pb", axis=1, tiled=True)
+    piece_k, piece_dk = jnp.split(
+        lax.all_gather(jnp.concatenate([keys, tangent_k], 0), "pb", axis=1, tiled=True),
+        [keys.shape[0]],
+        0,
+    )
     piece_v = lax.all_gather(values, "pb", axis=1, tiled=True)
     piece_dv = lax.all_gather(tangent_v, "pb", axis=1, tiled=True)
     shaped = (

time: 215 us -> 202 us (0.940)
  blocking collectives: 109 us -> 94.7 us
    all_gather x2 -> x1, blocking collectives: 29.9 us -> 14.9 us  [body(): lax.all_gather(jnp.concatenate([keys, tangent_k], 0), 'pb', axis=1, tiled...]
  transfers between devices with their start and end apart: 2 -> 2, of which waited for: 2 -> 2; matrix products, arithmetic and copies ran while one was open for 2% -> 3% of each run, Pallas kernels for 0% -> 0%
where the time goes in v1:
time: 202 us; the launch traced here: 201 us
  blocking collectives  94.7 us (47%)
  waiting for transfers between devices  43.1 us (21%)
  matrix products  23.9 us (12%)
  other arithmetic  14.4 us (7%)
  between operations  14.1 us (7%)
  local copies, waits for them, and re-layouts  10.7 us (5%)
    all_gather x2, waiting for transfers between devices, combined_all(): pieces = jax.tree.map(lambda part: lax.all_gather(part, axis), value)  42.4 us
    all_gather x3, blocking collectives, combined_all(): pieces = jax.tree.map(lambda part: lax.all_gather(part, axis), value)  26.4 us
    all_gather x1, blocking collectives, body(): piece_dv = lax.all_gather(tangent_v, 'pb', axis=1, tiled=True)  16.6 us
    all_gather x1, blocking collectives, body(): piece_v = lax.all_gather(values, 'pb', axis=1, tiled=True)  15.9 us
    all_gather x1, blocking collectives, body(): lax.all_gather(jnp.concatenate([keys, tangent_k], 0), 'pb', axis=1, tiled...  14.9 us
    add x7, other arithmetic, join_partials(): tnumer = first[3] * left[..., None] + second[3] * right[..., None]  11.9 us
    all_gather x1, blocking collectives, body(): lax.all_gather(tangent_q, 'ka', axis=1, tiled=True)  10.8 us
    all_gather x1, blocking collectives, body(): lax.all_gather(queries, 'ka', axis=1, tiled=True)  10.2 us
  transfers between devices with their start and end apart: 2, of which 2 were waited for; matrix products, arithmetic and copies ran while one was open for 3% of the time, Pallas kernels for 0%

profile of v1, /device:TPU:0, one launch (start us, length us, event | category | flops | bytes accessed | tf_op | source)
XLA Modules:
  0.0 201.2 jit_solution(11854006720202683521)
XLA Ops:
  7.3 15.9 %all_gather.32 = f32[1,512,128]{2,1,0:T(8,128)S(1)} all-gather(f32[1,128,128]{2,1,0:T(8,128)} %param.12), channel_id=1, replica_groups=mesh['pb'=4,'ka'=8] {'pb'}, dimensions={1}, use_global_device_ids=true | all-gather | bytes 327680 | tf_op jit(solution)/shard_map/all_gather | solution.py:51
  23.1 16.6 %all_gather.33 = f32[1,512,128]{2,1,0:T(8,128)} all-gather(f32[1,128,128]{2,1,0:T(8,128)} %param.15), channel_id=1, replica_groups=mesh['pb'=4,'ka'=8] {'pb'}, dimensions={1}, use_global_device_ids=true | all-gather | bytes 327680 | tf_op jit(solution)/shard_map/all_gather | solution.py:52
  40.6 14.9 %all_gather.31 = f32[2,512,128]{2,1,0:T(8,128)S(1)} all-gather(f32[2,128,128]{2,1,0:T(8,128)S(1)} %pad_maximum_fusion), channel_id=1, replica_groups=mesh['pb'=4,'ka'=8] {'pb'}, dimensions={1}, use_global_device_ids=true | all-gather | bytes 655360 | tf_op jit(solution)/shard_map/all_gather | solution.py:47
  55.5 10.2 %all_gather.30 = f32[1,1024,128]{2,1,0:T(8,128)S(1)} all-gather(f32[1,128,128]{2,1,0:T(8,128)} %param.10), channel_id=1, replica_groups=mesh['pb'=4,'ka'=8] {'ka'}, dimensions={1}, use_global_device_ids=true | all-gather | bytes 589824 | tf_op jit(solution)/shard_map/all_gather | solution.py:31
  65.7 10.8 %all_gather.34 = f32[1,1024,128]{2,1,0:T(8,128)} all-gather(f32[1,128,128]{2,1,0:T(8,128)} %param.13), channel_id=1, replica_groups=mesh['pb'=4,'ka'=8] {'ka'}, dimensions={1}, use_global_device_ids=true | all-gather | bytes 589824 | tf_op jit(solution)/shard_map/all_gather | solution.py:32
  76.5 24.6 %while.53 = (s32[]{:T(128)}, f32[2,512]{1,0:T(2,128)S(1)}, f32[2,512]{1,0:T(2,128)S(1)}, f32[2,512,128]{2,1,0:T(8,128)}, f32[2,512,128]{2,1,0:T(8,128)}, /*index...) while((s32[]{:T(128)}, f32[2,512]{1,0:T(2,128)S(1)}, ...), condition=%wide.region_4.5_spmd, body=%wide.region_0.4_spmd.sunk | while | flops 2419001344 | bytes 12892333 | solution.py:97
  76.5 1.9 fusion.66
  79.6 1.2 fusion.67
  80.9 2.8 %convolution_add_fusion.5 = f32[512,128]{1,0:T(8,128)S(1)} fusion(f32[512,128]{1,0:T(8,128)} %get-tuple-element.551, f32[512,512]{0,1:T(8,128)S(1)} %get-tuple-element.491, f32[512]{0:T(512)S(1)} %get-tuple-element.490, f32[512]{0:T(512)S(1)} %get-tuple-element.494), kind=kOutput, calls=%fused_computation.7.clone.1 | convolution fusion | flops 402980864 | bytes 1576960 | tf_op jit(solution)/shard_map/while/body/eval_jaxpr/while/body/eval_jaxpr/dot_general | solution.py:91
  83.7 2.5 %fusion.71 = f32[2,512,128]{2,1,0:T(8,128)} fusion(f32[2,512,128]{2,1,0:T(8,128)} %get-tuple-element.532, s32[]{:T(128)S(6)} %copy.19, f32[512,128]{1,0:T(8,128)S(1)} %convolution_add_fusion.5, f32[512,512]{0,1:T(8,128)S(1)} %get-tuple-element.495, f32[512,128]{1,0:T(8,128)S(1)} %get-tuple-element.550), kind=kOutput, calls=%fused_computation.6.clone.1 | convolution fusion | flops 402718720 | bytes 1835012 | tf_op jit(solution)/shard_map/while/body/eval_jaxpr/while/body/eval_jaxpr/dot_general | solution.py:92
  86.2 2.5 %fusion.70 = f32[2,512,128]{2,1,0:T(8,128)} fusion(f32[2,512,128]{2,1,0:T(8,128)} %get-tuple-element.531, s32[]{:T(128)S(6)} %copy.19, f32[512,128]{1,0:T(8,128)S(1)} %get-tuple-element.550, f32[512,512]{0,1:T(8,128)S(1)} %get-tuple-element.491, f32[512]{0:T(512)S(1)} %get-tuple-element.490, f32[512]{0:T(512)S(1)} %get-tuple-element.494), kind=kOutput, calls=%fused_computation.10.clone.1 | convolution fusion | flops 402980864 | bytes 1576964 | tf_op jit(solution)/shard_map/while/body/eval_jaxpr/while/body/eval_jaxpr/dot_general | solution.py:88
  88.8 1.9 fusion.66
  91.9 1.2 fusion.67
  93.2 2.8 %convolution_add_fusion.5 = f32[512,128]{1,0:T(8,128)S(1)} fusion(f32[512,128]{1,0:T(8,128)} %get-tuple-element.551, f32[512,512]{0,1:T(8,128)S(1)} %get-tuple-element.491, f32[512]{0:T(512)S(1)} %get-tuple-element.490, f32[512]{0:T(512)S(1)} %get-tuple-element.494), kind=kOutput, calls=%fused_computation.7.clone.1 | convolution fusion | flops 402980864 | bytes 1576960 | tf_op jit(solution)/shard_map/while/body/eval_jaxpr/while/body/eval_jaxpr/dot_general | solution.py:91
  96.0 2.5 %fusion.71 = f32[2,512,128]{2,1,0:T(8,128)} fusion(f32[2,512,128]{2,1,0:T(8,128)} %get-tuple-element.532, s32[]{:T(128)S(6)} %copy.19, f32[512,128]{1,0:T(8,128)S(1)} %convolution_add_fusion.5, f32[512,512]{0,1:T(8,128)S(1)} %get-tuple-element.495, f32[512,128]{1,0:T(8,128)S(1)} %get-tuple-element.550), kind=kOutput, calls=%fused_computation.6.clone.1 | convolution fusion | flops 402718720 | bytes 1835012 | tf_op jit(solution)/shard_map/while/body/eval_jaxpr/while/body/eval_jaxpr/dot_general | solution.py:92
  98.6 2.5 %fusion.70 = f32[2,512,128]{2,1,0:T(8,128)} fusion(f32[2,512,128]{2,1,0:T(8,128)} %get-tuple-element.531, s32[]{:T(128)S(6)} %copy.19, f32[512,128]{1,0:T(8,128)S(1)} %get-tuple-element.550, f32[512,512]{0,1:T(8,128)S(1)} %get-tuple-element.491, f32[512]{0:T(512)S(1)} %get-tuple-element.490, f32[512]{0:T(512)S(1)} %get-tuple-element.494), kind=kOutput, calls=%fused_computation.10.clone.1 | convolution fusion | flops 402980864 | bytes 1576964 | tf_op jit(solution)/shard_map/while/body/eval_jaxpr/while/body/eval_jaxpr/dot_general | solution.py:88
  101.9 8.8 %all_gather.36 = f32[8,1,1024]{2,1,0:T(1,128)S(1)} all-gather(f32[1,1,1024]{2,1,0:T(1,128)S(1)} %all_gather_reshape.16), channel_id=1, replica_groups=mesh['pb'=4,'ka'=8] {'ka'}, dimensions={0}, use_global_device_ids=true | all-gather | bytes 36864 | tf_op jit(solution)/shard_map/all_gather | solution.py:8
  110.7 8.6 %all_gather.35 = f32[8,1,1024]{2,1,0:T(1,128)S(1)} all-gather(f32[1,1,1024]{2,1,0:T(1,128)S(1)} %all_gather_reshape.15), channel_id=1, replica_groups=mesh['pb'=4,'ka'=8] {'ka'}, dimensions={0}, use_global_device_ids=true | all-gather | bytes 36864 | tf_op jit(solution)/shard_map/all_gather | solution.py:8
  119.3 9.0 %all_gather.39 = f32[8,1,1024]{2,1,0:T(1,128)S(1)} all-gather(f32[1,1,1024]{2,1,0:T(1,128)S(1)} %all_gather_reshape.19), channel_id=1, replica_groups=mesh['pb'=4,'ka'=8] {'ka'}, dimensions={0}, use_global_device_ids=true | all-gather | bytes 36864 | tf_op jit(solution)/shard_map/all_gather | solution.py:8
  128.3 9.1 %all-gather.5.cloned.1.call-done = f32[8,1,1024,128]{3,2,1,0:T(8,128)} async-done(((f32[1,1,1024,128]{3,2,1,0:T(8,128)}), f32[8,1,1024,128]{3,2,1,0:T(8,128)}) %all-gather.5.cloned.1.call-update) | async-done | bytes 4194320 | tf_op jit(solution)/shard_map/all_gather | solution.py:8
  137.4 4.1 %slice.48 = f32[7,1,1024,128]{3,2,1,0:T(8,128)} slice(f32[8,1,1024,128]{3,2,1,0:T(8,128)} %all-gather.5.cloned.1.call-done), slice={[1:8], [0:1], [0:1024], [0:128]} | slice | bytes 7340032 | tf_op jit(solution)/shard_map/slice | solution.py:10
  142.5 33.3 %all-gather.3.cloned.1.call-done = f32[8,1,1024,128]{3,2,1,0:T(8,128)} async-done(((f32[1,1,1024,128]{3,2,1,0:T(8,128)}), f32[8,1,1024,128]{3,2,1,0:T(8,128)}) %all-gather.3.cloned.1.call-update) | async-done | bytes 4194320 | tf_op jit(solution)/shard_map/all_gather | solution.py:8
  175.9 1.1 slice_bitcast_fusion.1
  177.0 4.1 %slice.47 = f32[7,1,1024,128]{3,2,1,0:T(8,128)} slice(f32[8,1,1024,128]{3,2,1,0:T(8,128)} %all-gather.3.cloned.1.call-done), slice={[1:8], [0:1], [0:1024], [0:128]} | slice | bytes 7340032 | tf_op jit(solution)/shard_map/slice | solution.py:10
  181.0 12.5 %while.54 = (s32[]{:T(128)}, f32[1,1024]{1,0:T(1,128)S(1)}, f32[1,1024]{1,0:T(1,128)S(1)}, f32[1,1024,128]{2,1,0:T(8,128)S(1)}, f32[1,1024,128]{2,1,0:T(8,128)S(...) while((s32[]{:T(128)}, f32[1,1024]{1,0:T(1,128)S(1)}, ...), condition=%wide.region_6.7_spmd, body=%wide.region_5.6_spmd.sunk | while | flops 795650 | bytes 3207305 | solution.py:11
  181.1 1.7 fusion.74
  182.9 1.7 fusion.74
  184.7 1.7 fusion.74
  186.5 1.7 fusion.74
  188.3 1.7 fusion.74
  190.0 1.7 fusion.74
  191.8 1.7 fusion.74
  (60 shorter events, 6.8 us)
Async XLA Ops:
  7.2 130.2 %all-gather.5.cloned.1.call-start = ((), (), s32[]{:S(2)}) async-start(), calls=%async_computation.1 | async-start | bytes 4718592 | tf_op jit(solution)/shard_map/all_gather | solution.py:8
  101.1 74.8 %all-gather.3.cloned.1.call-start = ((), (), s32[]{:S(2)}) async-start(), calls=%async_computation | async-start | bytes 4718592 | tf_op jit(solution)/shard_map/all_gather | solution.py:8
  110.7 31.8 %copy-start = (f32[8,1,1024]{2,1,0:T(1,128)}, f32[8,1,1024]{2,1,0:T(1,128)S(1)}, u32[]{:S(2)}) copy-start(f32[8,1,1024]{2,1,0:T(1,128)S(1)} %all_gather.36) | copy-start | bytes 98308
  119.3 23.2 %copy-start.1 = (f32[8,1,1024]{2,1,0:T(1,128)}, f32[8,1,1024]{2,1,0:T(1,128)S(1)}, u32[]{:S(2)}) copy-start(f32[8,1,1024]{2,1,0:T(1,128)S(1)} %all_gather.35) | copy-start | bytes 98308
  128.3 14.2 %copy-start.2 = (f32[8,1,1024]{2,1,0:T(1,128)}, f32[8,1,1024]{2,1,0:T(1,128)S(1)}, u32[]{:S(2)}) copy-start(f32[8,1,1024]{2,1,0:T(1,128)S(1)} %all_gather.39) | copy-start | bytes 98308
  175.9 5.2 %slice-start = ((f32[8,1,1024]{2,1,0:T(1,128)}), f32[7,1,1024]{2,1,0:T(1,128)S(1)}, s32[]{:S(2)}) async-start(f32[8,1,1024]{2,1,0:T(1,128)} %copy-done), calls=%async_computation.2 | async-start | bytes 57344 | tf_op jit(solution)/shard_map/slice | solution.py:10
  175.9 5.2 %slice-start.1 = ((f32[8,1,1024]{2,1,0:T(1,128)}), f32[7,1,1024]{2,1,0:T(1,128)S(1)}, s32[]{:S(2)}) async-start(f32[8,1,1024]{2,1,0:T(1,128)} %copy-done.1), calls=%async_computation.3 | async-start | bytes 57344 | tf_op jit(solution)/shard_map/slice | solution.py:10
  175.9 5.2 %slice-start.2 = ((f32[8,1,1024]{2,1,0:T(1,128)}), f32[7,1,1024]{2,1,0:T(1,128)S(1)}, s32[]{:S(2)}) async-start(f32[8,1,1024]{2,1,0:T(1,128)} %copy-done.2), calls=%async_computation.4 | async-start | bytes 57344 | tf_op jit(solution)/shard_map/slice | solution.py:10
Sparse Core Ops, SparseCore 0:
  101.2 36.0 all-gather.4
  139.2 36.5 all-gather.2
